TPU v7x, 32 devices: a whole 2x2x4 slice. The times are simulated.
32 devices in a mesh: gx: 2 (over y), gy: 4 (over z), gz: 4 (over x, core).
Axes of the slice: x: 2, y: 2, z: 4, core: 2. Of those that a mesh axis runs over, the one named last changes fastest.
Arguments:
- tokens: bfloat16 [512, 6144], P(('gx', 'gy'), 'gz'), may hold values from -6 to 6
- grad_out: bfloat16 [512, 6144], P(('gx', 'gy'), 'gz'), may hold values from -1.5 to 1.5
- w_in: bfloat16 [6144, 12288], P('gz', ('gy', 'gx')), may hold values from -0.078125 to 0.078125
- w_out: bfloat16 [12288, 6144], P(('gy', 'gx'), 'gz'), may hold values from -0.0546875 to 0.0546875
Outputs:
- mlp_out: bfloat16 [512, 6144], P(('gx', 'gy'), 'gz')
- tok_grad: bfloat16 [512, 6144], P(('gx', 'gy'), 'gz')
- win_grad: float32 [6144, 12288], P('gz', ('gy', 'gx'))
- wout_grad: float32 [12288, 6144], P(('gy', 'gx'), 'gz')
All inputs are finite; a program needn't handle non-finite values.
Results may differ from a plain program's by a relative error of at most 0.01.
Values may be sent and summed in bfloat16 or wider, within the bound.
A program may use at most 128 MiB of HBM per device.

v0:
```python
import math
import jax
import jax.numpy as jnp
from jax import lax
from jax.sharding import PartitionSpec as P


def gelu_slope(values):
    cdf = 0.5 * (1.0 + jax.scipy.special.erf(values * 0.7071067811865476))
    density = jnp.exp(-0.5 * values * values) * 0.3989422804014327
    return cdf + values * density


def contract_last(left, right):
    return lax.dot_general(
        left, right, (((1,), (1,)), ((), ())), preferred_element_type=jnp.float32
    )


def contract_first(left, right):
    return lax.dot_general(
        left, right, (((0,), (0,)), ((), ())), preferred_element_type=jnp.float32
    )


def per_device(tokens, grad_out, w_in, w_out):
    tok_rows, grad_rows = (
        lax.all_gather(tokens, "gy", axis=0, tiled=True),
        lax.all_gather(grad_out, "gy", axis=0, tiled=True),
    )
    win_tile, wout_tile = (
        lax.all_gather(w_in, "gx", axis=1, tiled=True),
        lax.all_gather(w_out, "gx", axis=0, tiled=True),
    )
    row_total = tok_rows.shape[0]
    block_scale = 1.0 / math.sqrt(row_total)
    pre_part = lax.psum_scatter(
        jnp.dot(tok_rows, win_tile, preferred_element_type=jnp.float32),
        "gz",
        scatter_dimension=0,
        tiled=True,
    )
    act_part = jax.nn.gelu(pre_part, approximate=False).astype(jnp.bfloat16)
    act_all = lax.all_gather(act_part, "gz", axis=0, tiled=True)
    mlp_out = lax.psum_scatter(
        jnp.dot(act_all, wout_tile, preferred_element_type=jnp.float32),
        "gy",
        scatter_dimension=0,
        tiled=True,
    ).astype(jnp.bfloat16)
    wout_grad = lax.psum_scatter(
        (contract_first(act_all, grad_rows) * block_scale).astype(jnp.bfloat16),
        "gx",
        scatter_dimension=0,
        tiled=True,
    ).astype(jnp.float32)
    dact_part = lax.psum_scatter(
        contract_last(grad_rows, wout_tile), "gz", scatter_dimension=0, tiled=True
    )
    dpre_part = (dact_part * gelu_slope(pre_part)).astype(jnp.bfloat16)
    dpre_all = lax.all_gather(dpre_part, "gz", axis=0, tiled=True)
    tok_grad = lax.psum_scatter(
        contract_last(dpre_all, win_tile), "gy", scatter_dimension=0, tiled=True
    ).astype(jnp.bfloat16)
    win_term = contract_first(tok_rows, dpre_all) * block_scale
    win_grad = lax.psum_scatter(
        win_term.astype(jnp.bfloat16), "gx", scatter_dimension=1, tiled=True
    ).astype(jnp.float32)
    return (mlp_out, tok_grad, win_grad, wout_grad)


def solution(mesh):
    in_specs = (
        P(("gx", "gy"), "gz"),
        P(("gx", "gy"), "gz"),
        P("gz", ("gy", "gx")),
        P(("gy", "gx"), "gz"),
    )
    out_specs = (
        P(("gx", "gy"), "gz"),
        P(("gx", "gy"), "gz"),
        P("gz", ("gy", "gx")),
        P(("gy", "gx"), "gz"),
    )
    return jax.shard_map(
        per_device, mesh=mesh, in_specs=in_specs, out_specs=out_specs, check_vma=False
    )
```

profile of v0, /device:TPU:0, one launch (start us, length us, event | category | flops | bytes accessed | tf_op | source)
XLA Modules:
  0.0 691.5 jit_solution(6097030964073734867)
XLA Ops:
  7.2 0.0 copy-start
  7.2 0.0 all-gather.9.cloned.1.call-start
  7.2 0.7 all-gather.9.cloned.1.call-update
  7.9 0.0 all-gather.5.cloned.1.call-start
  8.0 0.7 all-gather.5.cloned.1.call-update
  8.7 0.0 reduce-scatter.11.cloned.1.call-start
  8.7 0.0 copy-done
  8.7 21.3 %all_gather.22 = bf16[256,1536]{1,0:T(8,128)(2,1)S(1)} all-gather(bf16[64,1536]{1,0:T(8,128)(2,1)S(1)} %copy-done), channel_id=1, replica_groups=mesh['gx'=2,'gy'=4,'gz'=4] {'gy'}, dimensions={0}, use_global_device_ids=true | all-gather | bytes 983040 | tf_op jit(solution)/shard_map/all_gather | solution.py:29
  30.0 0.0 copy-start.1
  30.0 100.3 %all-gather.9.cloned.1.call-done = bf16[3072,1536]{1,0:T(8,128)(2,1)} async-done(((bf16[1536,1536]{1,0:T(8,128)(2,1)}), bf16[3072,1536]{1,0:T(8,128)(2,1)}) %all-gather.9.cloned.1.call-update) | async-done | bytes 9437200 | tf_op jit(solution)/shard_map/all_gather | solution.py:33
  130.3 8.0 %fusion.19 = f32[256,3072]{1,0:T(8,128)} fusion(bf16[256,1536]{1,0:T(8,128)(2,1)S(1)} %all_gather.22, bf16[3072,1536]{1,0:T(8,128)(2,1)} %all-gather.9.cloned.1.call-done), kind=kOutput, calls=%fused_computation.31 | convolution fusion | flops 2415919104 | bytes 13369344 | tf_op jit(solution)/shard_map/dot_general | solution.py:15
  138.3 0.0 reduce-scatter.11.cloned.1.call-update
  138.3 0.0 reduce-scatter.7.cloned.1.call-start
  138.3 0.0 copy-done.1
  138.3 19.6 %all_gather.18 = bf16[256,1536]{1,0:T(8,128)(2,1)S(1)} all-gather(bf16[64,1536]{1,0:T(8,128)(2,1)S(1)} %copy-done.1), channel_id=1, replica_groups=mesh['gx'=2,'gy'=4,'gz'=4] {'gy'}, dimensions={0}, use_global_device_ids=true | all-gather | bytes 983040 | tf_op jit(solution)/shard_map/all_gather | solution.py:28
  157.9 91.9 %all-gather.5.cloned.1.call-done = bf16[1536,3072]{1,0:T(8,128)(2,1)} async-done(((bf16[1536,1536]{1,0:T(8,128)(2,1)}), bf16[1536,3072]{1,0:T(8,128)(2,1)}) %all-gather.5.cloned.1.call-update) | async-done | bytes 9437200 | tf_op jit(solution)/shard_map/all_gather | solution.py:32
  249.8 7.9 %fusion.17 = f32[256,3072]{1,0:T(8,128)} fusion(bf16[256,1536]{1,0:T(8,128)(2,1)S(1)} %all_gather.18, bf16[1536,3072]{1,0:T(8,128)(2,1)} %all-gather.5.cloned.1.call-done), kind=kOutput, calls=%fused_computation.29 | convolution fusion | flops 2415919104 | bytes 13369344 | tf_op jit(solution)/shard_map/dot_general | solution.py:38
  257.8 0.0 reduce-scatter.7.cloned.1.call-update
  257.8 0.0 all-gather.11.cloned.1.call-start
  257.9 33.0 %reduce-scatter.11.cloned.1.call-done = f32[64,3072]{1,0:T(8,128)} async-done(((f32[256,3072]{1,0:T(8,128)}), f32[64,3072]{1,0:T(8,128)}) %reduce-scatter.11.cloned.1.call-update) | async-done | bytes 786448 | tf_op jit(solution)/shard_map/reduce_scatter | solution.py:57
  290.9 40.9 %reduce-scatter.7.cloned.1.call-done = f32[64,3072]{1,0:T(8,128)} async-done(((f32[256,3072]{1,0:T(8,128)}), f32[64,3072]{1,0:T(8,128)}) %reduce-scatter.7.cloned.1.call-update) | async-done | bytes 786448 | tf_op jit(solution)/shard_map/reduce_scatter | solution.py:37
  331.7 3.8 fusion.9
  335.6 0.0 all-gather.11.cloned.1.call-update
  335.6 0.0 all-gather.7.cloned.1.call-start
  335.6 0.5 all-gather.7.cloned.1.call-update
  336.2 0.0 reduce-scatter.13.cloned.1.call-start
  336.2 19.2 %all-gather.11.cloned.1.call-done = bf16[256,3072]{1,0:T(8,128)(2,1)} async-done(((bf16[64,3072]{1,0:T(8,128)(2,1)}), bf16[256,3072]{1,0:T(8,128)(2,1)}) %all-gather.11.cloned.1.call-update) | async-done | bytes 1572880 | tf_op jit(solution)/shard_map/all_gather | solution.py:61
  355.4 8.0 %fusion.20 = f32[256,1536]{1,0:T(8,128)} fusion(bf16[256,3072]{1,0:T(8,128)(2,1)} %all-gather.11.cloned.1.call-done, bf16[1536,3072]{1,0:T(8,128)(2,1)} %all-gather.5.cloned.1.call-done), kind=kOutput, calls=%fused_computation.32 | convolution fusion | flops 2415919104 | bytes 12582912 | tf_op jit(solution)/shard_map/dot_general | solution.py:15
  363.3 0.0 reduce-scatter.13.cloned.1.call-update
  363.4 0.0 reduce-scatter.9.cloned.1.call-start
  363.4 13.6 %all-gather.7.cloned.1.call-done = bf16[256,3072]{1,0:T(8,128)(2,1)} async-done(((bf16[64,3072]{1,0:T(8,128)(2,1)}), bf16[256,3072]{1,0:T(8,128)(2,1)}) %all-gather.7.cloned.1.call-update) | async-done | bytes 1572880 | tf_op jit(solution)/shard_map/all_gather | solution.py:44
  377.0 7.9 %fusion.18 = f32[256,1536]{1,0:T(8,128)} fusion(bf16[256,3072]{1,0:T(8,128)(2,1)} %all-gather.7.cloned.1.call-done, bf16[3072,1536]{1,0:T(8,128)(2,1)} %all-gather.9.cloned.1.call-done), kind=kOutput, calls=%fused_computation.30 | convolution fusion | flops 2415919104 | bytes 12582912 | tf_op jit(solution)/shard_map/dot_general | solution.py:46
  384.9 0.0 reduce-scatter.9.cloned.1.call-update
  385.0 0.0 copy-start.2
  385.0 0.0 reduce-scatter.17.cloned.1.call-start
  385.0 6.8 multiply_convert_fusion
  391.8 0.0 reduce-scatter.17.cloned.1.call-update
  391.8 0.2 reduce-scatter.15.cloned.1.call-start
  392.0 0.0 copy-done.2
  392.0 5.2 fusion
  397.2 0.0 reduce-scatter.15.cloned.1.call-update
  397.3 17.5 %reduce-scatter.13.cloned.1.call-done = f32[64,1536]{1,0:T(8,128)} async-done(((f32[256,1536]{1,0:T(8,128)}), f32[64,1536]{1,0:T(8,128)}) %reduce-scatter.13.cloned.1.call-update) | async-done | bytes 393232 | tf_op jit(solution)/shard_map/reduce_scatter | solution.py:62
  414.8 1.7 convert_element_type.30
  416.5 34.9 %reduce-scatter.9.cloned.1.call-done = f32[64,1536]{1,0:T(8,128)} async-done(((f32[256,1536]{1,0:T(8,128)}), f32[64,1536]{1,0:T(8,128)}) %reduce-scatter.9.cloned.1.call-update) | async-done | bytes 393232 | tf_op jit(solution)/shard_map/reduce_scatter | solution.py:45
  451.4 1.7 convert_element_type.28
  453.1 110.7 %reduce-scatter.17.cloned.1.call-done = bf16[1536,1536]{1,0:T(8,128)(2,1)} async-done(((bf16[3072,1536]{1,0:T(8,128)(2,1)}), bf16[1536,1536]{1,0:T(8,128)(2,1)}) %reduce-scatter.17.cloned.1.call-update) | async-done | bytes 4718608 | tf_op jit(solution)/shard_map/reduce_scatter | solution.py:51
  563.8 7.4 %convert_element_type.35 = f32[1536,1536]{1,0:T(8,128)} convert(bf16[1536,1536]{1,0:T(8,128)(2,1)} %reduce-scatter.17.cloned.1.call-done) | non-fusion elementwise | flops 2359296 | bytes 14155776 | tf_op jit(solution)/shard_map/convert_element_type | solution.py:56
  571.2 106.0 %reduce-scatter.15.cloned.1.call-done = bf16[1536,1536]{0,1:T(8,128)(2,1)} async-done(((bf16[1536,3072]{0,1:T(8,128)(2,1)}), bf16[1536,1536]{0,1:T(8,128)(2,1)}) %reduce-scatter.15.cloned.1.call-update) | async-done | bytes 4718608 | tf_op jit(solution)/shard_map/reduce_scatter | solution.py:66
  677.2 7.4 %copy.8 = f32[1536,1536]{1,0:T(8,128)} copy(bf16[1536,1536]{0,1:T(8,128)(2,1)} %reduce-scatter.15.cloned.1.call-done) | data formatting | bytes 14155776
Async XLA Ops:
  7.2 1.5 copy-start
  7.2 123.1 %all-gather.9.cloned.1.call-start = ((), (), s32[]{:S(2)}) async-start(), calls=%async_computation.9 | async-start | bytes 14155776 | tf_op jit(solution)/shard_map/all_gather | solution.py:33
  7.9 241.9 %all-gather.5.cloned.1.call-start = ((), (), s32[]{:S(2)}) async-start(), calls=%async_computation.6 | async-start | bytes 14155776 | tf_op jit(solution)/shard_map/all_gather | solution.py:32
  8.7 282.2 %reduce-scatter.11.cloned.1.call-start = ((), (), s32[]{:S(2)}) async-start(), calls=%async_computation.11 | async-start | bytes 3932160 | tf_op jit(solution)/shard_map/reduce_scatter | solution.py:57
  30.0 108.3 %copy-start.1 = (bf16[64,1536]{1,0:T(8,128)(2,1)S(1)}, bf16[64,1536]{1,0:T(8,128)(2,1)}, u32[]{:S(2)}) copy-start(bf16[64,1536]{1,0:T(8,128)(2,1)} %param.4) | copy-start | bytes 589828
  138.3 193.4 %reduce-scatter.7.cloned.1.call-start = ((), (), s32[]{:S(2)}) async-start(), calls=%async_computation.7 | async-start | bytes 3932160 | tf_op jit(solution)/shard_map/reduce_scatter | solution.py:37
  257.8 97.6 %all-gather.11.cloned.1.call-start = ((), (), s32[]{:S(2)}) async-start(), calls=%async_computation.12 | async-start | bytes 1966080 | tf_op jit(solution)/shard_map/all_gather | solution.py:61
  335.6 41.5 %all-gather.7.cloned.1.call-start = ((), (), s32[]{:S(2)}) async-start(), calls=%async_computation.8 | async-start | bytes 1966080 | tf_op jit(solution)/shard_map/all_gather | solution.py:44
  336.2 78.6 %reduce-scatter.13.cloned.1.call-start = ((), (), s32[]{:S(2)}) async-start(), calls=%async_computation.13 | async-start | bytes 1966080 | tf_op jit(solution)/shard_map/reduce_scatter | solution.py:62
  363.4 88.1 %reduce-scatter.9.cloned.1.call-start = ((), (), s32[]{:S(2)}) async-start(), calls=%async_computation.10 | async-start | bytes 1966080 | tf_op jit(solution)/shard_map/reduce_scatter | solution.py:45
  385.0 7.1 %copy-start.2 = (bf16[256,3072]{1,0:T(8,128)(2,1)S(1)}, bf16[256,3072]{1,0:T(8,128)(2,1)}, u32[]{:S(2)}) copy-start(bf16[256,3072]{1,0:T(8,128)(2,1)} %all-gather.11.cloned.1.call-done) | copy-start | bytes 4718596
  385.0 178.8 %reduce-scatter.17.cloned.1.call-start = ((), (), s32[]{:S(2)}) async-start(), calls=%async_computation.15 | async-start | bytes 14155776 | tf_op jit(solution)/shard_map/reduce_scatter | solution.py:51
  391.8 285.4 %reduce-scatter.15.cloned.1.call-start = ((), (), s32[]{:S(2)}) async-start(), calls=%async_computation.14 | async-start | bytes 14155776 | tf_op jit(solution)/shard_map/reduce_scatter | solution.py:66
Sparse Core Ops, SparseCore 0:
  9.5 120.6 all-gather.8
  131.8 117.9 all-gather.4
  252.9 37.8 reduce-scatter.10
  293.8 37.8 reduce-scatter.6
  335.7 19.6 all-gather.10
  357.4 19.6 all-gather.6
  379.3 35.4 reduce-scatter.12
  417.1 34.2 reduce-scatter.8
  454.3 109.4 reduce-scatter.16
  566.5 110.6 reduce-scatter.14
where the time goes:
time: 692 us; the launch traced here: 691 us
  waiting for transfers between devices  570 us (82%)
  matrix products  43.7 us (6%)
  blocking collectives  40.9 us (6%)
  other arithmetic  14.6 us (2%)
  between operations  14.2 us (2%)
  local copies, waits for them, and re-layouts  7.41 us (1%)
    reduce_scatter x1, waiting for transfers between devices, per_device(): lax.psum_scatter((contract_first(act_all, grad_rows) * block_scale).astyp...  111 us
    reduce_scatter x1, waiting for transfers between devices, per_device(): lax.psum_scatter(win_term.astype(jnp.bfloat16), 'gx', scatter_dimension=1...  106 us
    all_gather x1, waiting for transfers between devices, per_device(): lax.all_gather(w_out, 'gx', axis=0, tiled=True)  100 us
    all_gather x1, waiting for transfers between devices, per_device(): lax.all_gather(w_in, 'gx', axis=1, tiled=True)  91.9 us
    reduce_scatter x1, waiting for transfers between devices, per_device(): lax.psum_scatter(jnp.dot(tok_rows, win_tile, preferred_element_type=jnp.f...  40.9 us
    reduce_scatter x1, waiting for transfers between devices, per_device(): lax.psum_scatter(jnp.dot(act_all, wout_tile, preferred_element_type=jnp.f...  34.9 us
    reduce_scatter x1, waiting for transfers between devices, per_device(): lax.psum_scatter(contract_last(grad_rows, wout_tile), 'gz', scatter_dimen...  33 us
    all_gather x1, blocking collectives, per_device(): lax.all_gather(grad_out, 'gy', axis=0, tiled=True)  21.3 us
  transfers between devices with their start and end apart: 10, of which 10 were waited for; matrix products, arithmetic and copies ran while one was open for 8% of the time, Pallas kernels for 0%

commit v1 on v0

--- a/solution.py
+++ b/solution.py
@@ -3,6 +3,13 @@
 import jax.numpy as jnp
 from jax import lax
 from jax.sharding import PartitionSpec as P
+
+
+def exchange_gather(x, axis, dim):
+    devices = lax.axis_size(axis)
+    parts = jnp.stack([x for _ in range(devices)])
+    parts = lax.all_to_all(parts, axis, split_axis=0, concat_axis=0)
+    return jnp.concatenate(parts, axis=dim)
 
 
 def gelu_slope(values):
@@ -29,7 +36,7 @@
         lax.all_gather(grad_out, "gy", axis=0, tiled=True),
     )
     win_tile, wout_tile = (
-        lax.all_gather(w_in, "gx", axis=1, tiled=True),
+        exchange_gather(w_in, "gx", 1),
         lax.all_gather(w_out, "gx", axis=0, tiled=True),
     )
     row_total = tok_rows.shape[0]

time: 692 us -> 663 us (0.958)
  waiting for transfers between devices: 570 us -> 514 us
  other arithmetic: 14.6 us -> 24.5 us
  local copies, waits for them, and re-layouts: 7.41 us -> 16.4 us
  starting transfers between devices: 0.58 us -> 8.53 us
    all_to_all x0 -> x1, waiting for transfers between devices: none -> 177 us  [exchange_gather(): parts = lax.all_to_all(parts, axis, split_axis=0, concat_axis=0)]
    all_gather x1, waiting for transfers between devices: 100 us -> 0.01 us  [per_device(): lax.all_gather(w_out, 'gx', axis=0, tiled=True)]
    all_gather x1 -> x0, waiting for transfers between devices: 91.9 us -> none  [per_device(): lax.all_gather(w_in, 'gx', axis=1, tiled=True)]
    reduce_scatter x1, waiting for transfers between devices: 34.9 us -> 1.53 us  [per_device(): lax.psum_scatter(jnp.dot(act_all, wout_tile, preferred_element_type=jnp.f...]
    reduce_scatter x1, waiting for transfers between devices: 40.9 us -> 10.1 us  [per_device(): lax.psum_scatter(jnp.dot(tok_rows, win_tile, preferred_element_type=jnp.f...]
    reduce_scatter x1, waiting for transfers between devices: 17.5 us -> 34.9 us  [per_device(): lax.psum_scatter(contract_last(dpre_all, win_tile), 'gy', scatter_dimensi...]
    another operation x0 -> x1, other arithmetic: none -> 9.88 us  [exchange_gather(): parts = jnp.stack([x for _ in range(devices)])]
    unnamed x7 -> x11, local copies, waits for them, and re-layouts: 7.41 us -> 16.4 us
  transfers between devices with their start and end apart: 10 -> 10, of which waited for: 10 -> 9; matrix products, arithmetic and copies ran while one was open for 8% -> 11% of each run, Pallas kernels for 0% -> 0%
where the time goes in v1:
time: 663 us; the launch traced here: 662 us
  waiting for transfers between devices  514 us (78%)
  blocking collectives  41.6 us (6%)
  matrix products  41.3 us (6%)
  other arithmetic  24.5 us (4%)
  local copies, waits for them, and re-layouts  16.4 us (2%)
  between operations  15.6 us (2%)
  starting transfers between devices  8.53 us (1%)
    all_to_all x1, waiting for transfers between devices, exchange_gather(): parts = lax.all_to_all(parts, axis, split_axis=0, concat_axis=0)  177 us
    reduce_scatter x1, waiting for transfers between devices, per_device(): lax.psum_scatter(win_term.astype(jnp.bfloat16), 'gx', scatter_dimension=1...  111 us
    reduce_scatter x1, waiting for transfers between devices, per_device(): lax.psum_scatter((contract_first(act_all, grad_rows) * block_scale).astyp...  105 us
    reduce_scatter x1, waiting for transfers between devices, per_device(): lax.psum_scatter(contract_last(grad_rows, wout_tile), 'gz', scatter_dimen...  40.7 us
    reduce_scatter x1, waiting for transfers between devices, per_device(): lax.psum_scatter(contract_last(dpre_all, win_tile), 'gy', scatter_dimensi...  34.9 us
    all_gather x1, blocking collectives, per_device(): lax.all_gather(tokens, 'gy', axis=0, tiled=True)  22.1 us
    all_gather x1, blocking collectives, per_device(): lax.all_gather(grad_out, 'gy', axis=0, tiled=True)  19.6 us
    all_gather x1, waiting for transfers between devices, per_device(): act_all = lax.all_gather(act_part, 'gz', axis=0, tiled=True)  18.8 us
  transfers between devices with their start and end apart: 10, of which 9 were waited for; matrix products, arithmetic and copies ran while one was open for 11% of the time, Pallas kernels for 0%

profile of v1, /device:TPU:0, one launch (start us, length us, event | category | flops | bytes accessed | tf_op | source)
XLA Modules:
  0.0 662.0 jit_solution(3224236834754509280)
XLA Ops:
  8.0 0.0 all-gather.6.cloned.1.call-start
  8.0 0.7 all-gather.6.cloned.1.call-update
  8.7 6.6 copy.18
  15.3 9.9 %pad_maximum_fusion = bf16[2,1536,1536]{1,2,0:T(8,128)(2,1)} fusion(bf16[1,1536,1536]{1,2,0:T(8,128)(2,1)} %bitcast.22), kind=kLoop, calls=%fused_computation.3 | loop fusion | flops 4718592 | bytes 14155776 | tf_op jit(solution)/shard_map/stack | solution.py:10
  25.2 0.0 copy-start.1
  25.2 8.0 %all-to-all-start = ((bf16[2,1536,1536]{1,2,0:T(8,128)(2,1)}), bf16[2,1536,1536]{1,2,0:T(8,128)(2,1)}, u32[]{:S(2)}, u32[]{:S(2)}) async-start(bf16[2,1536,1536]{1,2,0:T(8,128)(2,1)} %pad_maximum_fusion), calls=%async_computation | async-start | bytes 18874368 | tf_op jit(solution)/shard_map/all_to_all | solution.py:11
  33.2 0.0 reduce-scatter.19.cloned.1.call-start
  33.2 0.0 copy-done.1
  33.3 22.1 %all_gather.15 = bf16[256,1536]{1,0:T(8,128)(2,1)} all-gather(bf16[64,1536]{1,0:T(8,128)(2,1)S(1)} %copy-done.1), channel_id=1, replica_groups=mesh['gx'=2,'gy'=4,'gz'=4] {'gy'}, dimensions={0}, use_global_device_ids=true | all-gather | bytes 983040 | tf_op jit(solution)/shard_map/all_gather | solution.py:35
  55.3 176.8 %all-to-all-done = bf16[2,1536,1536]{1,2,0:T(8,128)(2,1)} async-done(((bf16[2,1536,1536]{1,2,0:T(8,128)(2,1)}), bf16[2,1536,1536]{1,2,0:T(8,128)(2,1)}, u32[]{:S(2)}, u32[]{:S(2)}) %all-to-all-start) | async-done | bytes 9437216 | tf_op jit(solution)/shard_map/all_to_all | solution.py:11
  232.1 0.0 copy-start.2
  232.1 5.5 convolution_bitcast_fusion
  237.6 2.4 copy.29
  239.9 0.0 reduce-scatter.19.cloned.1.call-update
  240.0 0.0 reduce-scatter.21.cloned.1.call-start
  240.0 0.0 copy-done.2
  240.0 19.6 %all_gather.18 = bf16[256,1536]{1,0:T(8,128)(2,1)S(1)} all-gather(bf16[64,1536]{1,0:T(8,128)(2,1)S(1)} %copy-done.2), channel_id=1, replica_groups=mesh['gx'=2,'gy'=4,'gz'=4] {'gy'}, dimensions={0}, use_global_device_ids=true | all-gather | bytes 983040 | tf_op jit(solution)/shard_map/all_gather | solution.py:36
  259.6 0.0 all-gather.6.cloned.1.call-done
  259.6 8.0 %fusion.18 = f32[256,3072]{1,0:T(8,128)} fusion(bf16[256,1536]{1,0:T(8,128)(2,1)S(1)} %all_gather.18, bf16[3072,1536]{1,0:T(8,128)(2,1)} %all-gather.6.cloned.1.call-done), kind=kOutput, calls=%fused_computation.32 | convolution fusion | flops 2415919104 | bytes 13369344
  267.5 0.0 reduce-scatter.21.cloned.1.call-update
  267.6 0.0 all-gather.4.cloned.1.call-start
  267.6 10.1 %reduce-scatter.19.cloned.1.call-done = f32[64,3072]{1,0:T(8,128)} async-done(((f32[256,3072]{1,0:T(8,128)}), f32[64,3072]{1,0:T(8,128)}) %reduce-scatter.19.cloned.1.call-update) | async-done | bytes 786448 | tf_op jit(solution)/shard_map/reduce_scatter | solution.py:44
  277.8 40.7 %reduce-scatter.21.cloned.1.call-done = f32[64,3072]{1,0:T(8,128)} async-done(((f32[256,3072]{1,0:T(8,128)}), f32[64,3072]{1,0:T(8,128)}) %reduce-scatter.21.cloned.1.call-update) | async-done | bytes 786448 | tf_op jit(solution)/shard_map/reduce_scatter | solution.py:64
  318.5 3.8 fusion.9
  322.4 0.0 all-gather.4.cloned.1.call-update
  322.4 0.0 all-gather.8.cloned.1.call-start
  322.4 0.7 all-gather.8.cloned.1.call-update
  323.1 0.0 reduce-scatter.11.cloned.1.call-start
  323.2 18.8 %all-gather.4.cloned.1.call-done = bf16[256,3072]{1,0:T(8,128)(2,1)} async-done(((bf16[64,3072]{1,0:T(8,128)(2,1)}), bf16[256,3072]{1,0:T(8,128)(2,1)}) %all-gather.4.cloned.1.call-update) | async-done | bytes 1572880 | tf_op jit(solution)/shard_map/all_gather | solution.py:51
  342.0 7.9 %fusion.17 = f32[256,1536]{1,0:T(8,128)} fusion(bf16[256,3072]{1,0:T(8,128)(2,1)} %all-gather.4.cloned.1.call-done, bf16[3072,1536]{1,0:T(8,128)(2,1)} %all-gather.6.cloned.1.call-done), kind=kOutput, calls=%fused_computation.31 | convolution fusion | flops 2415919104 | bytes 12582912 | tf_op jit(solution)/shard_map/dot_general | solution.py:53
  349.9 0.0 reduce-scatter.11.cloned.1.call-update
  349.9 0.0 copy-start
  349.9 0.0 reduce-scatter.13.cloned.1.call-start
  350.0 13.7 %all-gather.8.cloned.1.call-done = bf16[256,3072]{1,0:T(8,128)(2,1)} async-done(((bf16[64,3072]{1,0:T(8,128)(2,1)}), bf16[256,3072]{1,0:T(8,128)(2,1)}) %all-gather.8.cloned.1.call-update) | async-done | bytes 1572880 | tf_op jit(solution)/shard_map/all_gather | solution.py:68
  363.7 8.1 %fusion.19 = f32[256,1536]{1,0:T(8,128)} fusion(bf16[256,3072]{1,0:T(8,128)(2,1)} %all-gather.8.cloned.1.call-done, bf16[1536,3072]{0,1:T(8,128)(2,1)} %bitcast.2), kind=kOutput, calls=%fused_computation.33 | convolution fusion | flops 2415919104 | bytes 12582912 | tf_op jit(solution)/shard_map/dot_general | solution.py:22
  371.7 0.0 reduce-scatter.13.cloned.1.call-update
  371.8 0.0 copy-start.3
  371.8 0.0 reduce-scatter.15.cloned.1.call-start
  371.8 0.0 copy-done
  371.8 6.7 %fusion = bf16[1536,3072]{0,1:T(8,128)(2,1)} fusion(bf16[256,3072]{1,0:T(8,128)(2,1)} %all-gather.8.cloned.1.call-done, bf16[256,1536]{1,0:T(8,128)(2,1)S(1)} %copy-done), kind=kOutput, calls=%fused_computation.2 | convolution fusion | flops 2425356288 | bytes 11796480 | tf_op jit(solution)/shard_map/dot_general | solution.py:28
  378.6 0.0 reduce-scatter.15.cloned.1.call-update
  378.6 0.2 reduce-scatter.17.cloned.1.call-start
  378.8 0.0 copy-done.3
  378.8 5.1 multiply_convert_fusion
  384.0 0.0 reduce-scatter.17.cloned.1.call-update
  384.0 1.5 reduce-scatter.11.cloned.1.call-done
  385.5 1.7 convert_element_type.28
  387.2 34.9 %reduce-scatter.13.cloned.1.call-done = f32[64,1536]{1,0:T(8,128)} async-done(((f32[256,1536]{1,0:T(8,128)}), f32[64,1536]{1,0:T(8,128)}) %reduce-scatter.13.cloned.1.call-update) | async-done | bytes 393232 | tf_op jit(solution)/shard_map/reduce_scatter | solution.py:69
  422.1 1.7 convert_element_type.30
  423.8 110.6 %reduce-scatter.15.cloned.1.call-done = bf16[1536,1536]{0,1:T(8,128)(2,1)} async-done(((bf16[1536,3072]{0,1:T(8,128)(2,1)}), bf16[1536,1536]{0,1:T(8,128)(2,1)}) %reduce-scatter.15.cloned.1.call-update) | async-done | bytes 4718608 | tf_op jit(solution)/shard_map/reduce_scatter | solution.py:73
  534.4 7.4 %copy.27 = f32[1536,1536]{1,0:T(8,128)} copy(bf16[1536,1536]{0,1:T(8,128)(2,1)} %reduce-scatter.15.cloned.1.call-done) | data formatting | bytes 14155776
  541.8 105.4 %reduce-scatter.17.cloned.1.call-done = bf16[1536,1536]{1,0:T(8,128)(2,1)} async-done(((bf16[3072,1536]{1,0:T(8,128)(2,1)}), bf16[1536,1536]{1,0:T(8,128)(2,1)}) %reduce-scatter.17.cloned.1.call-update) | async-done | bytes 4718608 | tf_op jit(solution)/shard_map/reduce_scatter | solution.py:58
  647.2 7.4 %convert_element_type.35 = f32[1536,1536]{1,0:T(8,128)} convert(bf16[1536,1536]{1,0:T(8,128)(2,1)} %reduce-scatter.17.cloned.1.call-done) | non-fusion elementwise | flops 2359296 | bytes 14155776 | tf_op jit(solution)/shard_map/convert_element_type | solution.py:63
Async XLA Ops:
  8.0 251.6 %all-gather.6.cloned.1.call-start = ((), (), s32[]{:S(2)}) async-start(), calls=%async_computation.8 | async-start | bytes 14155776 | tf_op jit(solution)/shard_map/all_gather | solution.py:40
  25.2 8.0 %copy-start.1 = (bf16[64,1536]{1,0:T(8,128)(2,1)S(1)}, bf16[64,1536]{1,0:T(8,128)(2,1)}, u32[]{:S(2)}) copy-start(bf16[64,1536]{1,0:T(8,128)(2,1)} %param.4) | copy-start | bytes 589828
  25.2 206.8 %all-to-all-start = ((bf16[2,1536,1536]{1,2,0:T(8,128)(2,1)}), bf16[2,1536,1536]{1,2,0:T(8,128)(2,1)}, u32[]{:S(2)}, u32[]{:S(2)}) async-start(bf16[2,1536,1536]{1,2,0:T(8,128)(2,1)} %pad_maximum_fusion), calls=%async_computation | async-start | bytes 18874368 | tf_op jit(solution)/shard_map/all_to_all | solution.py:11
  33.2 244.6 %reduce-scatter.19.cloned.1.call-start = ((), (), s32[]{:S(2)}) async-start(), calls=%async_computation.14 | async-start | bytes 3932160 | tf_op jit(solution)/shard_map/reduce_scatter | solution.py:44
  232.1 7.9 %copy-start.2 = (bf16[64,1536]{1,0:T(8,128)(2,1)S(1)}, bf16[64,1536]{1,0:T(8,128)(2,1)}, u32[]{:S(2)}) copy-start(bf16[64,1536]{1,0:T(8,128)(2,1)} %param.5) | copy-start | bytes 589828
  240.0 78.6 %reduce-scatter.21.cloned.1.call-start = ((), (), s32[]{:S(2)}) async-start(), calls=%async_computation.15 | async-start | bytes 3932160 | tf_op jit(solution)/shard_map/reduce_scatter | solution.py:64
  267.6 74.4 %all-gather.4.cloned.1.call-start = ((), (), s32[]{:S(2)}) async-start(), calls=%async_computation.7 | async-start | bytes 1966080 | tf_op jit(solution)/shard_map/all_gather | solution.py:51
  322.4 41.3 %all-gather.8.cloned.1.call-start = ((), (), s32[]{:S(2)}) async-start(), calls=%async_computation.10 | async-start | bytes 1966080 | tf_op jit(solution)/shard_map/all_gather | solution.py:68
  323.1 62.4 %reduce-scatter.11.cloned.1.call-start = ((), (), s32[]{:S(2)}) async-start(), calls=%async_computation.9 | async-start | bytes 1966080 | tf_op jit(solution)/shard_map/reduce_scatter | solution.py:52
  349.9 21.9 %copy-start = (bf16[256,1536]{1,0:T(8,128)(2,1)S(1)}, bf16[256,1536]{1,0:T(8,128)(2,1)}, u32[]{:S(2)}) copy-start(bf16[256,1536]{1,0:T(8,128)(2,1)} %all_gather.15) | copy-start | bytes 2359300
  349.9 72.2 %reduce-scatter.13.cloned.1.call-start = ((), (), s32[]{:S(2)}) async-start(), calls=%async_computation.11 | async-start | bytes 1966080 | tf_op jit(solution)/shard_map/reduce_scatter | solution.py:69
  371.8 7.1 %copy-start.3 = (bf16[256,3072]{1,0:T(8,128)(2,1)S(1)}, bf16[256,3072]{1,0:T(8,128)(2,1)}, u32[]{:S(2)}) copy-start(bf16[256,3072]{1,0:T(8,128)(2,1)} %all-gather.4.cloned.1.call-done) | copy-start | bytes 4718596
  371.8 162.6 %reduce-scatter.15.cloned.1.call-start = ((), (), s32[]{:S(2)}) async-start(), calls=%async_computation.12 | async-start | bytes 14155776 | tf_op jit(solution)/shard_map/reduce_scatter | solution.py:73
  378.6 268.6 %reduce-scatter.17.cloned.1.call-start = ((), (), s32[]{:S(2)}) async-start(), calls=%async_computation.13 | async-start | bytes 14155776 | tf_op jit(solution)/shard_map/reduce_scatter | solution.py:58
Sparse Core Ops, SparseCore 0:
  10.4 214.0 all-gather.5
  350.0 35.4 reduce-scatter.10
  387.8 34.2 reduce-scatter.12
  424.9 109.4 reduce-scatter.14
  536.5 110.6 reduce-scatter.16
Sparse Core Ops, SparseCore 1:
  240.0 37.7 reduce-scatter.18
  280.8 37.7 reduce-scatter.20
  322.5 19.5 all-gather.3
  344.2 19.5 all-gather.7
